TPU v7x, 32 devices: a whole 2x2x4 slice. The times are simulated.
32 devices in a mesh: ens: 4 (over z), shard: 4 (over y, core), tp: 2 (over x).
Axes of the slice: x: 2, y: 2, z: 4, core: 2. Of those that a mesh axis runs over, the one named last changes fastest.
Arguments:
- train_query: bfloat16 [14336, 4096], P(('ens', 'shard'), 'tp'), parts along dimension 0, may hold values from -0.09375 to 0.09375
- low_query: bfloat16 [14336, 32], P(('ens', 'shard')), parts along dimension 0, may hold values from -0.09375 to 0.09375
- high_query: bfloat16 [128, 4096], P('ens', 'tp'), parts along dimension 0, may hold values from -1 to 1
- train_key: bfloat16 [14336, 2048], P(('ens', 'shard'), 'tp'), parts along dimension 0, may hold values from -0.09375 to 0.09375
- low_key: bfloat16 [14336, 32], P(('ens', 'shard')), parts along dimension 0, may hold values from -0.09375 to 0.09375
- high_key: bfloat16 [128, 2048], P('ens', 'tp'), parts along dimension 0, may hold values from -1 to 1
- train_value: bfloat16 [14336, 2048], P(('ens', 'shard'), 'tp'), parts along dimension 0, may hold values from -0.09375 to 0.09375
- low_value: bfloat16 [14336, 32], P(('ens', 'shard')), parts along dimension 0, may hold values from -0.09375 to 0.09375
- high_value: bfloat16 [128, 2048], P('ens', 'tp'), parts along dimension 0, may hold values from -1 to 1
- train_mixed: bfloat16 [16384, 3584], P(('ens', 'tp'), 'shard'), parts along dimension 0, may hold values from -0.09375 to 0.09375
- low_mixed: bfloat16 [16384, 32], P(('ens', 'tp')), parts along dimension 0, may hold values from -0.09375 to 0.09375
- high_mixed: bfloat16 [128, 3584], P('ens', 'shard'), parts along dimension 0, may hold values from -1 to 1
- norm_train: float32 [14336], P(('ens', 'shard', 'tp')), parts along dimension 0, may hold values from 0.25 to 1.75
- norm_step: float32 [14336], P(('ens', 'shard', 'tp')), parts along dimension 0, may hold values from -0.3 to 0.3
Outputs:
- serve_query: bfloat16 [14336, 4096], P('ens', 'tp'), parts along dimension 0
- serve_key: bfloat16 [14336, 2048], P('ens', 'tp'), parts along dimension 0
- serve_value: bfloat16 [14336, 2048], P('ens', 'tp'), parts along dimension 0
- serve_mixed: bfloat16 [16384, 3584], P(('ens', 'tp')), parts along dimension 0
- serve_norm: bfloat16 [14336], P('ens'), parts along dimension 0
There are 4 independent parts, one for each index of `ens`. A program takes and returns all parts, laid end to end along the dimension named above; each array names one. Nothing has to cross between parts.
All inputs are finite; a program needn't handle non-finite values.
Results may differ from a plain program's by a relative error of at most 0.001.
Values may be sent and summed in bfloat16 or wider, within the bound.
A program may use at most 192 MiB of HBM per device.

v0:
```python
import jax
import jax.numpy as jnp
from jax import lax
from jax.sharding import PartitionSpec as P

mix_rate = 1.0


def per_device(
    train_query,
    low_query,
    high_query,
    train_key,
    low_key,
    high_key,
    train_value,
    low_value,
    high_value,
    train_mixed,
    low_mixed,
    high_mixed,
    norm_train,
    norm_step,
):
    (
        moved_query,
        moved_key,
        moved_value,
        moved_mixed,
        factor_query,
        factor_key,
        factor_value,
        factor_mixed,
    ) = (
        lax.all_gather(train_query, "shard", axis=0, tiled=True),
        lax.all_gather(train_key, "shard", axis=0, tiled=True),
        lax.all_gather(train_value, "shard", axis=0, tiled=True),
        lax.all_gather(train_mixed, "shard", axis=1, tiled=True),
        lax.all_gather(low_query, "shard", axis=0, tiled=True),
        lax.all_gather(low_key, "shard", axis=0, tiled=True),
        lax.all_gather(low_value, "shard", axis=0, tiled=True),
        lax.all_gather(high_mixed, "shard", axis=1, tiled=True),
    )
    fresh_query = moved_query.astype(jnp.float32) + mix_rate * jnp.dot(
        factor_query, high_query, preferred_element_type=jnp.float32
    )
    serve_query = fresh_query.astype(jnp.bfloat16)
    fresh_key = moved_key.astype(jnp.float32) + mix_rate * jnp.dot(
        factor_key, high_key, preferred_element_type=jnp.float32
    )
    serve_key = fresh_key.astype(jnp.bfloat16)
    fresh_value = moved_value.astype(jnp.float32) + mix_rate * jnp.dot(
        factor_value, high_value, preferred_element_type=jnp.float32
    )
    serve_value = fresh_value.astype(jnp.bfloat16)
    fresh_mixed = moved_mixed.astype(jnp.float32) + mix_rate * jnp.dot(
        low_mixed, factor_mixed, preferred_element_type=jnp.float32
    )
    serve_mixed = fresh_mixed.astype(jnp.bfloat16)
    serve_norm = lax.all_gather(
        (norm_train + norm_step).astype(jnp.bfloat16), ("shard", "tp"), axis=0, tiled=True
    )
    return (serve_query, serve_key, serve_value, serve_mixed, serve_norm)


def solution(mesh):
    return jax.shard_map(
        per_device,
        mesh=mesh,
        in_specs=(
            P(("ens", "shard"), "tp"),
            P(("ens", "shard"), None),
            P("ens", "tp"),
            P(("ens", "shard"), "tp"),
            P(("ens", "shard"), None),
            P("ens", "tp"),
            P(("ens", "shard"), "tp"),
            P(("ens", "shard"), None),
            P("ens", "tp"),
            P(("ens", "tp"), "shard"),
            P(("ens", "tp"), None),
            P("ens", "shard"),
            P(("ens", "shard", "tp")),
            P(("ens", "shard", "tp")),
        ),
        out_specs=(
            P("ens", "tp"),
            P("ens", "tp"),
            P("ens", "tp"),
            P(("ens", "tp"), None),
            P("ens"),
        ),
        check_vma=False,
    )
```

profile of v0, /device:TPU:0, one launch (start us, length us, event | category | flops | bytes accessed | tf_op | source)
XLA Modules:
  0.0 331.7 jit_solution(956389779975404595)
XLA Ops:
  7.2 0.0 all-gather.9.cloned.1.call-start
  7.2 0.7 all-gather.9.cloned.1.call-update
  7.9 0.0 all-gather.7.cloned.1.call-start
  8.0 0.7 all-gather.7.cloned.1.call-update
  8.7 0.0 all-gather.11.cloned.1.call-start
  8.7 0.7 all-gather.11.cloned.1.call-update
  9.4 0.0 all-gather.5.cloned.1.call-start
  9.5 0.5 all-gather.5.cloned.1.call-update
  10.0 1.2 dynamic-slice
  11.9 0.7 add_convert_fusion.4
  12.6 0.2 dynamic-update-slice
  12.8 16.3 %all-reduce = bf16[3584]{0:T(1024)(128)(2,1)} all-reduce(bf16[3584]{0:T(1024)(128)(2,1)S(1)} %dynamic-update-slice), channel_id=1, replica_groups=mesh['ens'=4,'shard'=4,'tp'=2] {'shard','tp'}, use_global_device_ids=true, to_apply=%add | all-reduce | flops 3584 | bytes 14336
  29.1 7.4 %all_gather.34 = bf16[32,3584]{1,0:T(8,128)(2,1)S(1)} all-gather(bf16[32,896]{1,0:T(8,128)(2,1)} %param.25), channel_id=1, replica_groups=mesh['ens'=4,'shard'=4,'tp'=2] {'shard'}, dimensions={1}, use_global_device_ids=true | all-gather | bytes 286720 | tf_op jit(solution)/shard_map/all_gather | solution.py:42
  36.5 7.6 %all_gather.28 = bf16[3584,32]{0,1:T(8,128)(2,1)S(1)} all-gather(bf16[896,32]{0,1:T(8,128)(2,1)} %param.15), channel_id=1, replica_groups=mesh['ens'=4,'shard'=4,'tp'=2] {'shard'}, dimensions={0}, use_global_device_ids=true | all-gather | bytes 286720 | tf_op jit(solution)/shard_map/all_gather | solution.py:39
  44.1 7.6 %all_gather.32 = bf16[3584,32]{0,1:T(8,128)(2,1)S(1)} all-gather(bf16[896,32]{0,1:T(8,128)(2,1)} %param.21), channel_id=1, replica_groups=mesh['ens'=4,'shard'=4,'tp'=2] {'shard'}, dimensions={0}, use_global_device_ids=true | all-gather | bytes 286720 | tf_op jit(solution)/shard_map/all_gather | solution.py:41
  51.7 7.6 %all_gather.30 = bf16[3584,32]{0,1:T(8,128)(2,1)S(1)} all-gather(bf16[896,32]{0,1:T(8,128)(2,1)} %param.18), channel_id=1, replica_groups=mesh['ens'=4,'shard'=4,'tp'=2] {'shard'}, dimensions={0}, use_global_device_ids=true | all-gather | bytes 286720 | tf_op jit(solution)/shard_map/all_gather | solution.py:40
  59.2 10.5 %all-gather.9.cloned.1.call-done = bf16[3584,1024]{1,0:T(8,128)(2,1)} async-done(((bf16[896,1024]{1,0:T(8,128)(2,1)}), bf16[3584,1024]{1,0:T(8,128)(2,1)}) %all-gather.9.cloned.1.call-update) | async-done | bytes 7340048 | tf_op jit(solution)/shard_map/all_gather | solution.py:37
  69.7 8.3 %add_convert_fusion.2 = bf16[3584,1024]{1,0:T(8,128)(2,1)} fusion(bf16[3584,1024]{1,0:T(8,128)(2,1)} %all-gather.9.cloned.1.call-done, bf16[3584,32]{0,1:T(8,128)(2,1)S(1)} %all_gather.32, bf16[32,1024]{1,0:T(8,128)(2,1)} %param.22), kind=kOutput, calls=%fused_computation.2 | convolution fusion | flops 245891072 | bytes 14974976 | tf_op jit(solution)/shard_map/dot_general | solution.py:52
  78.0 45.5 %all-gather.7.cloned.1.call-done = bf16[3584,1024]{1,0:T(8,128)(2,1)} async-done(((bf16[896,1024]{1,0:T(8,128)(2,1)}), bf16[3584,1024]{1,0:T(8,128)(2,1)}) %all-gather.7.cloned.1.call-update) | async-done | bytes 7340048 | tf_op jit(solution)/shard_map/all_gather | solution.py:36
  123.5 8.3 %add_convert_fusion.3 = bf16[3584,1024]{1,0:T(8,128)(2,1)} fusion(bf16[3584,1024]{1,0:T(8,128)(2,1)} %all-gather.7.cloned.1.call-done, bf16[3584,32]{0,1:T(8,128)(2,1)S(1)} %all_gather.30, bf16[32,1024]{1,0:T(8,128)(2,1)S(1)} %copy-done.2), kind=kOutput, calls=%fused_computation.3 | convolution fusion | flops 245891072 | bytes 14974976 | tf_op jit(solution)/shard_map/dot_general | solution.py:48
  131.8 87.2 %all-gather.11.cloned.1.call-done = bf16[2048,3584]{1,0:T(8,128)(2,1)} async-done(((bf16[2048,896]{1,0:T(8,128)(2,1)}), bf16[2048,3584]{1,0:T(8,128)(2,1)}) %all-gather.11.cloned.1.call-update) | async-done | bytes 14680080 | tf_op jit(solution)/shard_map/all_gather | solution.py:38
  219.0 11.9 %add_convert_fusion = bf16[2048,3584]{1,0:T(8,128)(2,1)} fusion(bf16[2048,3584]{1,0:T(8,128)(2,1)} %all-gather.11.cloned.1.call-done, bf16[2048,32]{0,1:T(8,128)(2,1)S(1)} %copy-done, bf16[32,3584]{1,0:T(8,128)(2,1)S(1)} %all_gather.34), kind=kOutput, calls=%fused_computation | convolution fusion | flops 491782144 | bytes 29720576 | tf_op jit(solution)/shard_map/dot_general | solution.py:56
  230.9 83.6 %all-gather.5.cloned.1.call-done = bf16[3584,2048]{1,0:T(8,128)(2,1)} async-done(((bf16[896,2048]{1,0:T(8,128)(2,1)}), bf16[3584,2048]{1,0:T(8,128)(2,1)}) %all-gather.5.cloned.1.call-update) | async-done | bytes 14680080 | tf_op jit(solution)/shard_map/all_gather | solution.py:35
  314.5 10.6 %add_convert_fusion.1 = bf16[3584,2048]{1,0:T(8,128)(2,1)} fusion(bf16[3584,2048]{1,0:T(8,128)(2,1)} %all-gather.5.cloned.1.call-done, bf16[3584,32]{0,1:T(8,128)(2,1)S(1)} %all_gather.28, bf16[32,2048]{1,0:T(8,128)(2,1)S(1)} %copy-done.1), kind=kOutput, calls=%fused_computation.1 | convolution fusion | flops 491782144 | bytes 29720576 | tf_op jit(solution)/shard_map/dot_general | solution.py:44
  (7 shorter events, 0.0 us)
Async XLA Ops:
  7.2 211.9 %copy-start = (bf16[2048,32]{0,1:T(8,128)(2,1)S(1)}, bf16[2048,32]{0,1:T(8,128)(2,1)}, u32[]{:S(2)}) copy-start(bf16[2048,32]{0,1:T(8,128)(2,1)} %param.24) | copy-start | bytes 393220
  7.2 116.4 %copy-start.2 = (bf16[32,1024]{1,0:T(8,128)(2,1)S(1)}, bf16[32,1024]{1,0:T(8,128)(2,1)}, u32[]{:S(2)}) copy-start(bf16[32,1024]{1,0:T(8,128)(2,1)} %param.19) | copy-start | bytes 196612
  7.2 62.5 %all-gather.9.cloned.1.call-start = ((), (), s32[]{:S(2)}) async-start(), calls=%async_computation.2 | async-start | bytes 9175040 | tf_op jit(solution)/shard_map/all_gather | solution.py:37
  7.9 115.6 %all-gather.7.cloned.1.call-start = ((), (), s32[]{:S(2)}) async-start(), calls=%async_computation.1 | async-start | bytes 9175040 | tf_op jit(solution)/shard_map/all_gather | solution.py:36
  8.7 210.4 %all-gather.11.cloned.1.call-start = ((), (), s32[]{:S(2)}) async-start(), calls=%async_computation.3 | async-start | bytes 18350080 | tf_op jit(solution)/shard_map/all_gather | solution.py:38
  9.4 305.1 %all-gather.5.cloned.1.call-start = ((), (), s32[]{:S(2)}) async-start(), calls=%async_computation | async-start | bytes 18350080 | tf_op jit(solution)/shard_map/all_gather | solution.py:35
  131.8 182.7 %copy-start.1 = (bf16[32,2048]{1,0:T(8,128)(2,1)S(1)}, bf16[32,2048]{1,0:T(8,128)(2,1)}, u32[]{:S(2)}) copy-start(bf16[32,2048]{1,0:T(8,128)(2,1)} %param.16) | copy-start | bytes 393220
Sparse Core Ops, SparseCore 0:
  9.6 60.1 all-gather.8
  71.3 52.2 all-gather.6
  125.1 93.8 all-gather.10
  220.4 93.9 all-gather.4
where the time goes:
time: 332 us
  waiting for transfers between devices  229 us (69%)
  blocking collectives  46.4 us (14%)
  matrix products  39 us (12%)
  between operations  14.4 us (4%)
    all_gather x1, waiting for transfers between devices, per_device(): lax.all_gather(train_mixed, 'shard', axis=1, tiled=True)  87.2 us
    all_gather x1, waiting for transfers between devices, per_device(): lax.all_gather(train_query, 'shard', axis=0, tiled=True)  83.6 us
    all_gather x1, waiting for transfers between devices, per_device(): lax.all_gather(train_key, 'shard', axis=0, tiled=True)  45.5 us
    unnamed x1, blocking collectives  16.3 us
    dot_general x1, matrix products, per_device(): jnp.dot(low_mixed, factor_mixed, preferred_element_type=jnp.float32)  11.9 us
    dot_general x1, matrix products, per_device(): jnp.dot(factor_query, high_query, preferred_element_type=jnp.float32)  10.6 us
    all_gather x1, waiting for transfers between devices, per_device(): lax.all_gather(train_value, 'shard', axis=0, tiled=True)  10.5 us
    dot_general x1, matrix products, per_device(): jnp.dot(factor_value, high_value, preferred_element_type=jnp.float32)  8.26 us
  transfers between devices with their start and end apart: 4, of which 4 were waited for; matrix products, arithmetic and copies ran while one was open for 9% of the time, Pallas kernels for 0%

commit v1 on v0

v1 whole, which is shorter than its diff:
```python
import functools

import jax
import jax.numpy as jnp
from jax import lax
from jax.experimental import pallas as pl
from jax.experimental.pallas import tpu as pltpu
from jax.sharding import PartitionSpec as P


mix_rate = 1.0
UNIT = 128

PLAN = (
    ("key", 0, 1),
    ("key", 1, 7),
    ("query", 0, 4),
    ("query", 4, 7),
    ("value", 0, 7),
    ("mixed", 0, 8),
    ("mixed", 8, 14),
    ("mixed", 14, 16),
)


def merged(train, low, high):
    fresh = train.astype(jnp.float32) + mix_rate * jnp.dot(low, high, preferred_element_type=jnp.float32)
    return fresh.astype(jnp.bfloat16)


def merge_kernel(train_ref, turned_ref, high_ref, out_ref):
    update = lax.dot_general(
        turned_ref[...], high_ref[...], (((0,), (0,)), ((), ())), preferred_element_type=jnp.float32
    )
    out_ref[...] = (train_ref[...].astype(jnp.float32) + mix_rate * update).astype(out_ref.dtype)


def merge_piece(train, turned, high, first, last):
    columns, rank = train.shape[1], turned.shape[0]
    rows = (last - first) * UNIT
    return pl.pallas_call(
        merge_kernel,
        grid=(last - first,),
        in_specs=[
            pl.BlockSpec((UNIT, columns), lambda i: (first + i, 0)),
            pl.BlockSpec((rank, UNIT), lambda i: (0, first + i)),
            pl.BlockSpec((rank, columns), lambda i: (0, 0)),
        ],
        out_specs=pl.BlockSpec((UNIT, columns), lambda i: (i, 0)),
        out_shape=jax.ShapeDtypeStruct((rows, columns), jnp.bfloat16),
        cost_estimate=pl.CostEstimate(
            flops=2 * rows * columns * rank, bytes_accessed=4 * rows * columns, transcendentals=0
        ),
        name="merge",
    )(train, turned, high)


def place_kernel(masks, row, by_rows, aliased, *refs):
    n = len(masks)
    sources = refs[:n]
    out_ref, staged, in_sems, out_sems = refs[n + aliased :]
    rows, columns = sources[0].shape
    me = lax.axis_index("shard")
    loads = []
    for j in range(n):
        load = pltpu.make_async_copy(sources[j], staged.at[j], in_sems.at[j])
        load.start()
        loads.append(load)
    stores = []
    for j, mask in enumerate(masks):
        low, high = me % 2, me // 2
        owner = (high + mask // 2 - 2 * high * (mask // 2)) * 2 + (low + mask % 2 - 2 * low * (mask % 2))
        if by_rows:
            span = out_ref.shape[0] // 4
            target = out_ref.at[pl.ds(pl.multiple_of(owner * span + row, UNIT), rows), :]
        else:
            target = out_ref.at[pl.ds(row, rows), pl.ds(pl.multiple_of(owner * columns, 128), columns)]
        store = pltpu.make_async_copy(staged.at[j], target, out_sems.at[j])
        loads[j].wait()
        store.start()
        stores.append(store)
    for store in stores:
        store.wait()


def place(out, out_shape, pieces, row, by_rows):
    masks = tuple(mask for mask, _ in pieces)
    arrays = [array for _, array in pieces]
    n = len(arrays)
    rows, columns = arrays[0].shape
    aliased = out is not None
    return pl.pallas_call(
        functools.partial(place_kernel, masks, row, by_rows, aliased),
        in_specs=[pl.BlockSpec(memory_space=pltpu.HBM)] * (n + aliased),
        out_specs=pl.BlockSpec(memory_space=pltpu.HBM),
        out_shape=out_shape,
        scratch_shapes=[
            pltpu.VMEM((n, rows, columns), jnp.bfloat16),
            pltpu.SemaphoreType.DMA((n,)),
            pltpu.SemaphoreType.DMA((n,)),
        ],
        input_output_aliases={n: 0} if aliased else {},
        cost_estimate=pl.CostEstimate(flops=0, bytes_accessed=4 * n * rows * columns, transcendentals=0),
        name="place",
    )(*arrays, *([out] if aliased else []))


def swap(array, mask):
    return lax.ppermute(array, "shard", [(s, s ^ mask) for s in range(4)])


def gathered_norm(norm_train, norm_step):
    fresh = (norm_train + norm_step).astype(jnp.bfloat16)
    return lax.all_gather(fresh, ("shard", "tp"), axis=0, tiled=True)


def after(array, earlier):
    return lax.optimization_barrier((array, earlier))[0]


def exchange(weights, norm_train, norm_step):
    turned = {name: low.T for name, (_, low, _, _) in weights.items()}
    shapes = {
        name: jax.ShapeDtypeStruct(
            (train.shape[0] * (4 if by_rows else 1), train.shape[1] * (1 if by_rows else 4)), jnp.bfloat16
        )
        for name, (train, _, _, by_rows) in weights.items()
    }
    outs = {name: None for name in weights}
    own, across, beside, both = [], [], [], []
    for k, (name, first, last) in enumerate(PLAN):
        train, _, high, _ = weights[name]
        own.append(merge_piece(train, turned[name], high, first, last))
        across.append(swap(own[k], 2))
        beside.append(swap(own[k], 1))
    serve_norm = gathered_norm(after(norm_train, own[-1]), norm_step)
    across[1] = after(across[1], serve_norm)
    for k in range(len(PLAN)):
        both.append(swap(across[k], 1))
    for pieces in (
        [((0, own[k]), (1, beside[k])) for k in range(len(PLAN))],
        [((2, across[k]), (3, both[k])) for k in range(len(PLAN))],
    ):
        for k, (name, first, _) in enumerate(PLAN):
            outs[name] = place(outs[name], shapes[name], pieces[k], first * UNIT, weights[name][3])
    return outs, serve_norm


def per_device(
    fits,
    train_query,
    low_query,
    high_query,
    train_key,
    low_key,
    high_key,
    train_value,
    low_value,
    high_value,
    train_mixed,
    low_mixed,
    high_mixed,
    norm_train,
    norm_step,
):
    weights = {
        "query": (train_query, low_query, high_query, True),
        "key": (train_key, low_key, high_key, True),
        "value": (train_value, low_value, high_value, True),
        "mixed": (train_mixed, low_mixed, high_mixed, False),
    }
    if fits:
        outs, serve_norm = exchange(weights, norm_train, norm_step)
    else:
        serve_norm = gathered_norm(norm_train, norm_step)
        outs = {
            name: lax.all_gather(merged(train, low, high), "shard", axis=0 if by_rows else 1, tiled=True)
            for name, (train, low, high, by_rows) in weights.items()
        }
    return (outs["query"], outs["key"], outs["value"], outs["mixed"], serve_norm)


def solution(mesh):
    fits = mesh.shape["shard"] == 4 and mesh.shape["tp"] == 2
    return jax.shard_map(
        functools.partial(per_device, fits),
        mesh=mesh,
        in_specs=(
            P(("ens", "shard"), "tp"),
            P(("ens", "shard"), None),
            P("ens", "tp"),
            P(("ens", "shard"), "tp"),
            P(("ens", "shard"), None),
            P("ens", "tp"),
            P(("ens", "shard"), "tp"),
            P(("ens", "shard"), None),
            P("ens", "tp"),
            P(("ens", "tp"), "shard"),
            P(("ens", "tp"), None),
            P("ens", "shard"),
            P(("ens", "shard", "tp")),
            P(("ens", "shard", "tp")),
        ),
        out_specs=(
            P("ens", "tp"),
            P("ens", "tp"),
            P("ens", "tp"),
            P(("ens", "tp"), None),
            P("ens"),
        ),
        check_vma=False,
    )
```

time: 332 us -> 303 us (0.913)
  Pallas kernels: 0 us -> 81.9 us
  waiting for transfers between devices: 229 us -> 187 us
  matrix products: 39 us -> 0 us
  blocking collectives: 46.4 us -> 14.7 us
  starting transfers between devices: 0.15 us -> 14.3 us
  between operations: 14.4 us -> 1.59 us
    all_gather x4 -> x0, waiting for transfers between devices: 227 us -> none  [the longest x1 87.2 us: per_device(): lax.all_gather(train_mixed, 'shard', axis=1, tiled=True)]
    ppermute x0 -> x24, waiting for transfers between devices: none -> 187 us  [swap(): return lax.ppermute(array, 'shard', [(s, s ^ mask) for s in range(4)])]
    pallas_call x0 -> x24, Pallas kernels: none -> 81.9 us  [the longest x16 46.5 us: place(): pl.pallas_call(functools.partial(place_kernel, masks, row, by_rows, alias...]
    dot_general x4 -> x0, matrix products: 39 us -> none  [the longest x1 11.9 us: per_device(): jnp.dot(low_mixed, factor_mixed, preferred_element_type=jnp.float32)]
    all_gather x4 -> x0, blocking collectives: 30.1 us -> none  [the longest x1 7.55 us: per_device(): lax.all_gather(low_value, 'shard', axis=0, tiled=True)]
    ppermute x0 -> x24, starting transfers between devices: none -> 14.3 us  [swap(): return lax.ppermute(array, 'shard', [(s, s ^ mask) for s in range(4)])]
  transfers between devices with their start and end apart: 4 -> 24, of which waited for: 4 -> 7; matrix products, arithmetic and copies ran while one was open for 9% -> 0% of each run, Pallas kernels for 0% -> 24%
where the time goes in v1:
time: 303 us; the launch traced here: 302 us
  waiting for transfers between devices  187 us (62%)
  Pallas kernels  81.9 us (27%)
  blocking collectives  14.7 us (5%)
  starting transfers between devices  14.3 us (5%)
  local copies, waits for them, and re-layouts  3.13 us (1%)
    ppermute x24, waiting for transfers between devices, swap(): return lax.ppermute(array, 'shard', [(s, s ^ mask) for s in range(4)])  187 us
    pallas_call x16, Pallas kernels, place(): pl.pallas_call(functools.partial(place_kernel, masks, row, by_rows, alias...  46.5 us
    pallas_call x8, Pallas kernels, merge_piece(): pl.pallas_call(merge_kernel, grid=(last - first,), in_specs=[pl.BlockSpec...  35.5 us
    unnamed x1, blocking collectives  14.7 us
    ppermute x24, starting transfers between devices, swap(): return lax.ppermute(array, 'shard', [(s, s ^ mask) for s in range(4)])  14.3 us
  transfers between devices with their start and end apart: 24, of which 7 were waited for; matrix products, arithmetic and copies ran while one was open for 0% of the time, Pallas kernels for 24%

profile of v1, /device:TPU:0, one launch (start us, length us, event | category | flops | bytes accessed | tf_op | source)
XLA Modules:
  0.0 302.2 jit_solution(11642596320236692284)
XLA Ops:
  0.6 5.2 %merge.14.refs_0_ = bf16[768,896]{1,0:T(8,128)(2,1)} custom-call(bf16[2048,896]{1,0:T(8,128)(2,1)} %train_ref.15, bf16[32,2048]{1,0:T(8,128)(2,1)} %bitcast.5, bf16[32,896]{1,0:T(8,128)(2,1)} %high_ref.15), custom_call_target="tpu_custom_call" | custom-call | flops 44040192 | bytes 2752512 | tf_op jit(solution)/shard_map/merge/pallas_call | solution.py:41
  13.6 5.2 %merge.10.refs_0_ = bf16[768,1024]{1,0:T(8,128)(2,1)} custom-call(bf16[896,1024]{1,0:T(8,128)(2,1)} %train_ref.12, bf16[32,896]{1,0:T(8,128)(2,1)} %bitcast.11, bf16[32,1024]{1,0:T(8,128)(2,1)} %high_ref.12), custom_call_target="tpu_custom_call" | custom-call | flops 50331648 | bytes 3145728 | tf_op jit(solution)/shard_map/merge/pallas_call | solution.py:41
  19.3 28.0 %collective-permute-done.8.refs_0_ = bf16[128,1024]{1,0:T(8,128)(2,1)S(1)} collective-permute-done((bf16[128,1024]{1,0:T(8,128)(2,1)}, bf16[128,1024]{1,0:T(8,128)(2,1)S(1)}, u32[]{:S(2)}, u32[]{:S(2)}) %collective-permute-start.8) | collective-permute-done | bytes 262176 | tf_op jit(solution)/shard_map/ppermute | solution.py:109
  49.1 10.2 %collective-permute-done.15.refs_0_ = bf16[256,896]{1,0:T(8,128)(2,1)S(1)} collective-permute-done((bf16[256,896]{1,0:T(8,128)(2,1)S(1)}, bf16[256,896]{1,0:T(8,128)(2,1)S(1)}, u32[]{:S(2)}, u32[]{:S(2)}) %collective-permute-start.15) | collective-permute-done | bytes 458784 | tf_op jit(solution)/shard_map/ppermute | solution.py:109
  60.8 3.8 %merge.8.refs_0_ = bf16[384,2048]{1,0:T(8,128)(2,1)} custom-call(bf16[896,2048]{1,0:T(8,128)(2,1)} %train_ref.9, bf16[32,896]{1,0:T(8,128)(2,1)} %bitcast.8, bf16[32,2048]{1,0:T(8,128)(2,1)} %high_ref.9), custom_call_target="tpu_custom_call" | custom-call | flops 50331648 | bytes 3145728 | tf_op jit(solution)/shard_map/merge/pallas_call | solution.py:41
  64.7 6.5 %merge.15.refs_0_ = bf16[1024,896]{1,0:T(8,128)(2,1)} custom-call(bf16[2048,896]{1,0:T(8,128)(2,1)} %train_ref.15, bf16[32,2048]{1,0:T(8,128)(2,1)} %bitcast.7, bf16[32,896]{1,0:T(8,128)(2,1)} %high_ref.15), custom_call_target="tpu_custom_call" | custom-call | flops 58720256 | bytes 3670016 | tf_op jit(solution)/shard_map/merge/pallas_call | solution.py:41
  73.7 4.6 %merge.9.refs_0_ = bf16[512,2048]{1,0:T(8,128)(2,1)} custom-call(bf16[896,2048]{1,0:T(8,128)(2,1)} %train_ref.9, bf16[32,896]{1,0:T(8,128)(2,1)} %bitcast.9, bf16[32,2048]{1,0:T(8,128)(2,1)} %high_ref.9), custom_call_target="tpu_custom_call" | custom-call | flops 67108864 | bytes 4194304 | tf_op jit(solution)/shard_map/merge/pallas_call | solution.py:41
  78.3 18.6 %collective-permute-done.6.refs_0_ = bf16[768,1024]{1,0:T(8,128)(2,1)} collective-permute-done((bf16[768,1024]{1,0:T(8,128)(2,1)}, bf16[768,1024]{1,0:T(8,128)(2,1)}, u32[]{:S(2)}, u32[]{:S(2)}) %collective-permute-start.6) | collective-permute-done | bytes 1572896 | tf_op jit(solution)/shard_map/ppermute | solution.py:109
  98.4 5.9 %merge.13.refs_0_ = bf16[896,1024]{1,0:T(8,128)(2,1)} custom-call(bf16[896,1024]{1,0:T(8,128)(2,1)} %train_ref.13, bf16[32,896]{1,0:T(8,128)(2,1)} %bitcast.12, bf16[32,1024]{1,0:T(8,128)(2,1)} %high_ref.13), custom_call_target="tpu_custom_call" | custom-call | flops 58720256 | bytes 3670016 | tf_op jit(solution)/shard_map/merge/pallas_call | solution.py:41
  104.3 26.3 %collective-permute-done.refs_0_ = bf16[384,2048]{1,0:T(8,128)(2,1)} collective-permute-done((bf16[384,2048]{1,0:T(8,128)(2,1)}, bf16[384,2048]{1,0:T(8,128)(2,1)}, u32[]{:S(2)}, u32[]{:S(2)}) %collective-permute-start) | collective-permute-done | bytes 1572896 | tf_op jit(solution)/shard_map/ppermute | solution.py:109
  133.6 14.7 %all-reduce = bf16[3584]{0:T(1024)(128)(2,1)} all-reduce(bf16[3584]{0:T(1024)(128)(2,1)S(1)} %dynamic-update-slice), channel_id=1, replica_groups=mesh['ens'=4,'shard'=4,'tp'=2] {'shard','tp'}, use_global_device_ids=true, to_apply=%add | all-reduce | flops 3584 | bytes 14336
  148.3 21.9 %collective-permute-done.19.refs_0_ = bf16[1024,896]{1,0:T(8,128)(2,1)} collective-permute-done((bf16[1024,896]{1,0:T(8,128)(2,1)}, bf16[1024,896]{1,0:T(8,128)(2,1)}, u32[]{:S(2)}, u32[]{:S(2)}) %collective-permute-start.19) | collective-permute-done | bytes 1835040 | tf_op jit(solution)/shard_map/ppermute | solution.py:109
  170.8 44.4 %collective-permute-done.2.refs_0_ = bf16[512,2048]{1,0:T(8,128)(2,1)} collective-permute-done((bf16[512,2048]{1,0:T(8,128)(2,1)}, bf16[512,2048]{1,0:T(8,128)(2,1)}, u32[]{:S(2)}, u32[]{:S(2)}) %collective-permute-start.2) | collective-permute-done | bytes 2097184 | tf_op jit(solution)/shard_map/ppermute | solution.py:109
  215.2 37.0 %collective-permute-done.12.refs_0_ = bf16[896,1024]{1,0:T(8,128)(2,1)} collective-permute-done((bf16[896,1024]{1,0:T(8,128)(2,1)}, bf16[896,1024]{1,0:T(8,128)(2,1)}, u32[]{:S(2)}, u32[]{:S(2)}) %collective-permute-start.12) | collective-permute-done | bytes 1835040 | tf_op jit(solution)/shard_map/ppermute | solution.py:109
  255.1 3.1 %place.21.refs_2_ = bf16[3584,1024]{1,0:T(8,128)(2,1)} custom-call(bf16[768,1024]{1,0:T(8,128)(2,1)} %merge.10.refs_0_, bf16[768,1024]{1,0:T(8,128)(2,1)} %collective-permute-done.10.refs_1_, bf16[3584,1024]{1,0:T(8,128)(2,1)} %place.20.refs_2_), custom_call_target="tpu_custom_call", output_to_operand_aliasing={{}: (2, {})} | custom-call | bytes 6291456 | tf_op jit(solution)/shard_map/place/pallas_call | solution.py:92
  260.0 3.4 %place.26.refs_2_ = bf16[2048,3584]{1,0:T(8,128)(2,1)} custom-call(bf16[1024,896]{1,0:T(8,128)(2,1)} %merge.15.refs_0_, bf16[1024,896]{1,0:T(8,128)(2,1)} %collective-permute-done.23.refs_1_), custom_call_target="tpu_custom_call" | custom-call | bytes 7340032 | tf_op jit(solution)/shard_map/place/pallas_call | solution.py:92
  263.4 3.4 %place.24.refs_2_ = bf16[3584,1024]{1,0:T(8,128)(2,1)} custom-call(bf16[896,1024]{1,0:T(8,128)(2,1)} %merge.13.refs_0_, bf16[896,1024]{1,0:T(8,128)(2,1)} %collective-permute-done.14.refs_1_), custom_call_target="tpu_custom_call" | custom-call | bytes 7340032 | tf_op jit(solution)/shard_map/place/pallas_call | solution.py:92
  271.6 3.6 %place.16.refs_2_ = bf16[3584,2048]{1,0:T(8,128)(2,1)} custom-call(bf16[512,2048]{1,0:T(8,128)(2,1)} %merge.9.refs_0_, bf16[512,2048]{1,0:T(8,128)(2,1)} %collective-permute-done.5.refs_1_), custom_call_target="tpu_custom_call" | custom-call | bytes 8388608 | tf_op jit(solution)/shard_map/place/pallas_call | solution.py:92
  275.3 3.1 %place.17.refs_2_ = bf16[3584,2048]{1,0:T(8,128)(2,1)} custom-call(bf16[384,2048]{1,0:T(8,128)(2,1)} %merge.8.refs_0_, bf16[384,2048]{1,0:T(8,128)(2,1)} %collective-permute-done.4.refs_1_, bf16[3584,2048]{1,0:T(8,128)(2,1)} %place.16.refs_2_), custom_call_target="tpu_custom_call", output_to_operand_aliasing={{}: (2, {})} | custom-call | bytes 6291456 | tf_op jit(solution)/shard_map/place/pallas_call | solution.py:92
  278.4 3.1 %place.23 = bf16[3584,1024]{1,0:T(8,128)(2,1)} custom-call(bf16[768,1024]{1,0:T(8,128)(2,1)} %collective-permute-done.6.refs_0_, bf16[768,1024]{1,0:T(8,128)(2,1)} %collective-permute-done.7.refs_1_, bf16[3584,1024]{1,0:T(8,128)(2,1)} %place.22.refs_2_), custom_call_target="tpu_custom_call", output_to_operand_aliasing={{}: (2, {})} | custom-call | bytes 6291456 | tf_op jit(solution)/shard_map/place/pallas_call | solution.py:92
  281.5 3.4 %place.29.refs_2_ = bf16[2048,3584]{1,0:T(8,128)(2,1)} custom-call(bf16[1024,896]{1,0:T(8,128)(2,1)} %collective-permute-done.19.refs_0_, bf16[1024,896]{1,0:T(8,128)(2,1)} %collective-permute-done.20.refs_1_, bf16[2048,3584]{1,0:T(8,128)(2,1)} %place.28.refs_2_), custom_call_target="tpu_custom_call", output_to_operand_aliasing={{}: (2, {})} | custom-call | bytes 7340032 | tf_op jit(solution)/shard_map/place/pallas_call | solution.py:92
  290.9 3.4 %place.25 = bf16[3584,1024]{1,0:T(8,128)(2,1)} custom-call(bf16[896,1024]{1,0:T(8,128)(2,1)} %collective-permute-done.12.refs_0_, bf16[896,1024]{1,0:T(8,128)(2,1)} %collective-permute-done.13.refs_1_, bf16[3584,1024]{1,0:T(8,128)(2,1)} %place.24.refs_2_), custom_call_target="tpu_custom_call", output_to_operand_aliasing={{}: (2, {})} | custom-call | bytes 7340032 | tf_op jit(solution)/shard_map/place/pallas_call | solution.py:92
  294.3 3.6 %place.18.refs_2_ = bf16[3584,2048]{1,0:T(8,128)(2,1)} custom-call(bf16[512,2048]{1,0:T(8,128)(2,1)} %collective-permute-done.2.refs_0_, bf16[512,2048]{1,0:T(8,128)(2,1)} %collective-permute-done.3.refs_1_, bf16[3584,2048]{1,0:T(8,128)(2,1)} %place.17.refs_2_), custom_call_target="tpu_custom_call", output_to_operand_aliasing={{}: (2, {})} | custom-call | bytes 8388608 | tf_op jit(solution)/shard_map/place/pallas_call | solution.py:92
  299.1 3.1 %place.19 = bf16[3584,2048]{1,0:T(8,128)(2,1)} custom-call(bf16[384,2048]{1,0:T(8,128)(2,1)} %collective-permute-done.refs_0_, bf16[384,2048]{1,0:T(8,128)(2,1)} %copy-done.3, bf16[3584,2048]{1,0:T(8,128)(2,1)} %place.18.refs_2_), custom_call_target="tpu_custom_call", output_to_operand_aliasing={{}: (2, {})} | custom-call | bytes 6291456 | tf_op jit(solution)/shard_map/place/pallas_call | solution.py:92
  (77 shorter events, 34.9 us)
Async XLA Ops:
  5.9 65.4 %collective-permute-start.22 = (bf16[768,896]{1,0:T(8,128)(2,1)}, bf16[768,896]{1,0:T(8,128)(2,1)}, u32[]{:S(2)}, u32[]{:S(2)}) collective-permute-start(bf16[768,896]{1,0:T(8,128)(2,1)} %merge.14.refs_0_), channel_id=1, source_target_pairs={{0,2},{2,0},{4,6},{6,4},{1,3},{3,1},{5,7},{7,5},{8,10},{10,8},{12,... | collective-permute-start | bytes 4128776 | tf_op jit(solution)/shard_map/ppermute | solution.py:109
  8.3 10.6 %collective-permute-start.11 = (bf16[128,1024]{1,0:T(8,128)(2,1)}, bf16[128,1024]{1,0:T(8,128)(2,1)S(1)}, u32[]{:S(2)}, u32[]{:S(2)}) collective-permute-start(bf16[128,1024]{1,0:T(8,128)(2,1)} %merge.12.refs_0_), channel_id=1, source_target_pairs={{0,2},{2,0},{4,6},{6,4},{1,3},{3,1},{5,7},{7,5},{8,10},{10,8},{12,... | collective-permute-start | bytes 786440 | tf_op jit(solution)/shard_map/ppermute | solution.py:109
  8.4 63.3 %collective-permute-start.17 = (bf16[768,896]{1,0:T(8,128)(2,1)S(1)}, bf16[768,896]{1,0:T(8,128)(2,1)}, u32[]{:S(2)}, u32[]{:S(2)}) collective-permute-start(bf16[768,896]{1,0:T(8,128)(2,1)S(1)} %copy-done.1), channel_id=1, source_target_pairs={{0,4},{2,6},{4,0},{6,2},{1,5},{3,7},{5,1},{7,3},{8,12},{10,14},{12... | collective-permute-start | bytes 4128776 | tf_op jit(solution)/shard_map/ppermute | solution.py:109
  11.3 36.1 %collective-permute-start.8 = (bf16[128,1024]{1,0:T(8,128)(2,1)}, bf16[128,1024]{1,0:T(8,128)(2,1)S(1)}, u32[]{:S(2)}, u32[]{:S(2)}) collective-permute-start(bf16[128,1024]{1,0:T(8,128)(2,1)} %merge.12.refs_0_), channel_id=1, source_target_pairs={{0,4},{2,6},{4,0},{6,2},{1,5},{3,7},{5,1},{7,3},{8,12},{10,14},{12... | collective-permute-start | bytes 786440 | tf_op jit(solution)/shard_map/ppermute | solution.py:109
  13.6 35.5 %collective-permute-start.21 = (bf16[256,896]{1,0:T(8,128)(2,1)}, bf16[256,896]{1,0:T(8,128)(2,1)S(1)}, u32[]{:S(2)}, u32[]{:S(2)}) collective-permute-start(bf16[256,896]{1,0:T(8,128)(2,1)} %merge.11.refs_0_), channel_id=1, source_target_pairs={{0,2},{2,0},{4,6},{6,4},{1,3},{3,1},{5,7},{7,5},{8,10},{10,8},{12,... | collective-permute-start | bytes 1376264 | tf_op jit(solution)/shard_map/ppermute | solution.py:109
  18.8 53.4 %collective-permute-start.10 = (bf16[768,1024]{1,0:T(8,128)(2,1)}, bf16[768,1024]{1,0:T(8,128)(2,1)}, u32[]{:S(2)}, u32[]{:S(2)}) collective-permute-start(bf16[768,1024]{1,0:T(8,128)(2,1)} %merge.10.refs_0_), channel_id=1, source_target_pairs={{0,2},{2,0},{4,6},{6,4},{1,3},{3,1},{5,7},{7,5},{8,10},{10,8},{12,... | collective-permute-start | bytes 4718600 | tf_op jit(solution)/shard_map/ppermute | solution.py:109
  47.4 12.0 %collective-permute-start.15 = (bf16[256,896]{1,0:T(8,128)(2,1)S(1)}, bf16[256,896]{1,0:T(8,128)(2,1)S(1)}, u32[]{:S(2)}, u32[]{:S(2)}) collective-permute-start(bf16[256,896]{1,0:T(8,128)(2,1)S(1)} %copy-done.2), channel_id=1, source_target_pairs={{0,4},{2,6},{4,0},{6,2},{1,5},{3,7},{5,1},{7,3},{8,12},{10,14},{12... | collective-permute-start | bytes 1376264 | tf_op jit(solution)/shard_map/ppermute | solution.py:109
  49.1 15.5 %collective-permute-start.9 = (bf16[128,1024]{1,0:T(8,128)(2,1)S(1)}, bf16[128,1024]{1,0:T(8,128)(2,1)}, u32[]{:S(2)}, u32[]{:S(2)}) collective-permute-start(bf16[128,1024]{1,0:T(8,128)(2,1)S(1)} %collective-permute-done.8.refs_0_), channel_id=1, source_target_pairs={{0,2},{2,0},{4,6},{6,4},{1,3},{3,1},{5,7},{7,5},{8,10},{10,8},{12,... | collective-permute-start | bytes 786440 | tf_op jit(solution)/shard_map/ppermute | solution.py:109
  59.3 37.6 %collective-permute-start.6 = (bf16[768,1024]{1,0:T(8,128)(2,1)}, bf16[768,1024]{1,0:T(8,128)(2,1)}, u32[]{:S(2)}, u32[]{:S(2)}) collective-permute-start(bf16[768,1024]{1,0:T(8,128)(2,1)} %merge.10.refs_0_), channel_id=1, source_target_pairs={{0,4},{2,6},{4,0},{6,2},{1,5},{3,7},{5,1},{7,3},{8,12},{10,14},{12... | collective-permute-start | bytes 4718600 | tf_op jit(solution)/shard_map/ppermute | solution.py:109
  64.6 39.7 %collective-permute-start.4 = (bf16[384,2048]{1,0:T(8,128)(2,1)}, bf16[384,2048]{1,0:T(8,128)(2,1)}, u32[]{:S(2)}, u32[]{:S(2)}) collective-permute-start(bf16[384,2048]{1,0:T(8,128)(2,1)} %merge.8.refs_0_), channel_id=1, source_target_pairs={{0,2},{2,0},{4,6},{6,4},{1,3},{3,1},{5,7},{7,5},{8,10},{10,8},{12,... | collective-permute-start | bytes 4718600 | tf_op jit(solution)/shard_map/ppermute | solution.py:109
  71.2 60.9 %collective-permute-start.23 = (bf16[1024,896]{1,0:T(8,128)(2,1)}, bf16[1024,896]{1,0:T(8,128)(2,1)}, u32[]{:S(2)}, u32[]{:S(2)}) collective-permute-start(bf16[1024,896]{1,0:T(8,128)(2,1)} %merge.15.refs_0_), channel_id=1, source_target_pairs={{0,2},{2,0},{4,6},{6,4},{1,3},{3,1},{5,7},{7,5},{8,10},{10,8},{12,... | collective-permute-start | bytes 5505032 | tf_op jit(solution)/shard_map/ppermute | solution.py:109
  71.7 58.9 %collective-permute-start = (bf16[384,2048]{1,0:T(8,128)(2,1)}, bf16[384,2048]{1,0:T(8,128)(2,1)}, u32[]{:S(2)}, u32[]{:S(2)}) collective-permute-start(bf16[384,2048]{1,0:T(8,128)(2,1)} %merge.8.refs_0_), channel_id=1, source_target_pairs={{0,4},{2,6},{4,0},{6,2},{1,5},{3,7},{5,1},{7,3},{8,12},{10,14},{12... | collective-permute-start | bytes 4718600 | tf_op jit(solution)/shard_map/ppermute | solution.py:109
  72.3 98.0 %collective-permute-start.19 = (bf16[1024,896]{1,0:T(8,128)(2,1)}, bf16[1024,896]{1,0:T(8,128)(2,1)}, u32[]{:S(2)}, u32[]{:S(2)}) collective-permute-start(bf16[1024,896]{1,0:T(8,128)(2,1)} %merge.15.refs_0_), channel_id=1, source_target_pairs={{0,4},{2,6},{4,0},{6,2},{1,5},{3,7},{5,1},{7,3},{8,12},{10,14},{12... | collective-permute-start | bytes 5505032 | tf_op jit(solution)/shard_map/ppermute | solution.py:109
  96.9 118.3 %collective-permute-start.2 = (bf16[512,2048]{1,0:T(8,128)(2,1)}, bf16[512,2048]{1,0:T(8,128)(2,1)}, u32[]{:S(2)}, u32[]{:S(2)}) collective-permute-start(bf16[512,2048]{1,0:T(8,128)(2,1)} %merge.9.refs_0_), channel_id=1, source_target_pairs={{0,4},{2,6},{4,0},{6,2},{1,5},{3,7},{5,1},{7,3},{8,12},{10,14},{12... | collective-permute-start | bytes 6291464 | tf_op jit(solution)/shard_map/ppermute | solution.py:109
  104.3 66.0 %collective-permute-start.14 = (bf16[896,1024]{1,0:T(8,128)(2,1)}, bf16[896,1024]{1,0:T(8,128)(2,1)}, u32[]{:S(2)}, u32[]{:S(2)}) collective-permute-start(bf16[896,1024]{1,0:T(8,128)(2,1)} %merge.13.refs_0_), channel_id=1, source_target_pairs={{0,2},{2,0},{4,6},{6,4},{1,3},{3,1},{5,7},{7,5},{8,10},{10,8},{12,... | collective-permute-start | bytes 5505032 | tf_op jit(solution)/shard_map/ppermute | solution.py:109
  130.6 121.7 %collective-permute-start.12 = (bf16[896,1024]{1,0:T(8,128)(2,1)}, bf16[896,1024]{1,0:T(8,128)(2,1)}, u32[]{:S(2)}, u32[]{:S(2)}) collective-permute-start(bf16[896,1024]{1,0:T(8,128)(2,1)} %merge.13.refs_0_), channel_id=1, source_target_pairs={{0,4},{2,6},{4,0},{6,2},{1,5},{3,7},{5,1},{7,3},{8,12},{10,14},{12... | collective-permute-start | bytes 5505032 | tf_op jit(solution)/shard_map/ppermute | solution.py:109
  132.1 120.2 %collective-permute-start.5 = (bf16[512,2048]{1,0:T(8,128)(2,1)S(1)}, bf16[512,2048]{1,0:T(8,128)(2,1)}, u32[]{:S(2)}, u32[]{:S(2)}) collective-permute-start(bf16[512,2048]{1,0:T(8,128)(2,1)S(1)} %copy-done), channel_id=1, source_target_pairs={{0,2},{2,0},{4,6},{6,4},{1,3},{3,1},{5,7},{7,5},{8,10},{10,8},{12,... | collective-permute-start | bytes 6291464 | tf_op jit(solution)/shard_map/ppermute | solution.py:109
  170.3 82.5 %collective-permute-start.7 = (bf16[768,1024]{1,0:T(8,128)(2,1)}, bf16[768,1024]{1,0:T(8,128)(2,1)}, u32[]{:S(2)}, u32[]{:S(2)}) collective-permute-start(bf16[768,1024]{1,0:T(8,128)(2,1)} %collective-permute-done.6.refs_0_), channel_id=1, source_target_pairs={{0,2},{2,0},{4,6},{6,4},{1,3},{3,1},{5,7},{7,5},{8,10},{10,8},{12,... | collective-permute-start | bytes 4718600 | tf_op jit(solution)/shard_map/ppermute | solution.py:109
  170.3 82.6 %collective-permute-start.20 = (bf16[1024,896]{1,0:T(8,128)(2,1)}, bf16[1024,896]{1,0:T(8,128)(2,1)}, u32[]{:S(2)}, u32[]{:S(2)}) collective-permute-start(bf16[1024,896]{1,0:T(8,128)(2,1)} %collective-permute-done.19.refs_0_), channel_id=1, source_target_pairs={{0,2},{2,0},{4,6},{6,4},{1,3},{3,1},{5,7},{7,5},{8,10},{10,8},{12,... | collective-permute-start | bytes 5505032 | tf_op jit(solution)/shard_map/ppermute | solution.py:109
  215.2 79.0 %collective-permute-start.3 = (bf16[512,2048]{1,0:T(8,128)(2,1)}, bf16[512,2048]{1,0:T(8,128)(2,1)}, u32[]{:S(2)}, u32[]{:S(2)}) collective-permute-start(bf16[512,2048]{1,0:T(8,128)(2,1)} %collective-permute-done.2.refs_0_), channel_id=1, source_target_pairs={{0,2},{2,0},{4,6},{6,4},{1,3},{3,1},{5,7},{7,5},{8,10},{10,8},{12,... | collective-permute-start | bytes 6291464 | tf_op jit(solution)/shard_map/ppermute | solution.py:109
  252.3 38.6 %collective-permute-start.13 = (bf16[896,1024]{1,0:T(8,128)(2,1)}, bf16[896,1024]{1,0:T(8,128)(2,1)}, u32[]{:S(2)}, u32[]{:S(2)}) collective-permute-start(bf16[896,1024]{1,0:T(8,128)(2,1)} %collective-permute-done.12.refs_0_), channel_id=1, source_target_pairs={{0,2},{2,0},{4,6},{6,4},{1,3},{3,1},{5,7},{7,5},{8,10},{10,8},{12,... | collective-permute-start | bytes 5505032 | tf_op jit(solution)/shard_map/ppermute | solution.py:109
  252.3 45.6 %collective-permute-start.1 = (bf16[384,2048]{1,0:T(8,128)(2,1)}, bf16[384,2048]{1,0:T(8,128)(2,1)S(1)}, u32[]{:S(2)}, u32[]{:S(2)}) collective-permute-start(bf16[384,2048]{1,0:T(8,128)(2,1)} %collective-permute-done.refs_0_), channel_id=1, source_target_pairs={{0,2},{2,0},{4,6},{6,4},{1,3},{3,1},{5,7},{7,5},{8,10},{10,8},{12,... | collective-permute-start | bytes 4718600 | tf_op jit(solution)/shard_map/ppermute | solution.py:109
  252.8 32.1 %collective-permute-start.18 = (bf16[768,896]{1,0:T(8,128)(2,1)}, bf16[768,896]{1,0:T(8,128)(2,1)S(1)}, u32[]{:S(2)}, u32[]{:S(2)}) collective-permute-start(bf16[768,896]{1,0:T(8,128)(2,1)} %collective-permute-done.17.refs_0_), channel_id=1, source_target_pairs={{0,2},{2,0},{4,6},{6,4},{1,3},{3,1},{5,7},{7,5},{8,10},{10,8},{12,... | collective-permute-start | bytes 4128776 | tf_op jit(solution)/shard_map/ppermute | solution.py:109
  252.9 36.0 %collective-permute-start.16 = (bf16[256,896]{1,0:T(8,128)(2,1)S(1)}, bf16[256,896]{1,0:T(8,128)(2,1)}, u32[]{:S(2)}, u32[]{:S(2)}) collective-permute-start(bf16[256,896]{1,0:T(8,128)(2,1)S(1)} %collective-permute-done.15.refs_0_), channel_id=1, source_target_pairs={{0,2},{2,0},{4,6},{6,4},{1,3},{3,1},{5,7},{7,5},{8,10},{10,8},{12,... | collective-permute-start | bytes 1376264 | tf_op jit(solution)/shard_map/ppermute | solution.py:109
  (12 other events, 528.3 us)
